TPU v7x, 128 devices: a whole 4x4x4 slice. The times are simulated.
128 devices in a mesh: dp: 8 (over y, core), tp: 16 (over z, x).
Axes of the slice: x: 4, y: 4, z: 4, core: 2. Of those that a mesh axis runs over, the one named last changes fastest.
Arguments:
- tokens: bfloat16 [10240, 6144], P(('dp', 'tp')), parts along dimension 0, may hold values from -6 to 6
- ln_gain: float32 [6144], replicated, may hold values from 0.25 to 1.75
- ln_bias: float32 [6144], replicated, may hold values from -1.75 to 1.75
- w_qkv: bfloat16 [6144, 3, 6144], P(None, None, 'tp'), may hold values from -0.45927933 to 0.45927933
- b_qkv: float32 [3, 6144], P(None, 'tp'), may hold values from -3 to 3
- w_out: bfloat16 [6144, 6144], P('tp'), may hold values from -0.078125 to 0.078125
- b_out: float32 [6144], replicated, may hold values from -1.25 to 1.25
- kv_cache: bfloat16 [2, 96, 128, 6144], P(None, 'dp', None, 'tp'), parts along dimension 1, may hold values from -6 to 6
- page_table: int32 [8, 10], P('dp'), parts along dimension 0, may hold values from 0 to 11, as said below
- lengths: int32 [8], P('dp'), parts along dimension 0, may hold values from 641 to 1280
Outputs:
- attn_out: bfloat16 [10240, 6144], P(('dp', 'tp')), parts along dimension 0
- kv_cache_out: bfloat16 [2, 96, 128, 6144], P(None, 'dp', None, 'tp'), parts along dimension 1
There are 8 independent parts, one for each index of `dp`. A program takes and returns all parts, laid end to end along the dimension named above; an argument that names none is the same for every part. Nothing has to cross between parts.
Inputs may be any that keep to these rules, and one draw needn't show every extreme that they name: `page_table`: no slot is named twice within a part.
All inputs are finite; a program needn't handle non-finite values.
Results may differ from a plain program's by a relative error of at most 0.015.
The roundings to bfloat16 on the way count: a program that leaves them out, or rounds other values in their place, can miss the bound.
Values may be sent and summed in bfloat16 or wider, within the bound.
A program may use at most 128 MiB of HBM per device.

v0:
```python
import math
import jax
import jax.numpy as jnp
from jax import lax
from jax.sharding import PartitionSpec as P

HD = 128
SEQS = 1
norm_eps = 1e-05


def layer_norm(token_rows, gain_row, shift_row):
    floats = token_rows.astype(jnp.float32)
    center = jnp.mean(floats, axis=-1, keepdims=True)
    spread = jnp.mean(jnp.square(floats - center), axis=-1, keepdims=True)
    return ((floats - center) * lax.rsqrt(spread + norm_eps) * gain_row + shift_row).astype(
        jnp.bfloat16
    )


def attend(queries, keys, values, lengths):
    seq_count, seq_len, head_count, head_dim = queries.shape
    block_len = math.gcd(seq_len, 512)
    score_scale = 1.0 / math.sqrt(head_dim)
    key_pos = jnp.arange(seq_len, dtype=jnp.int32)

    def one_sequence(inputs):
        seq_query, seq_key, seq_value, length = inputs
        blocks = seq_query.reshape(seq_len // block_len, block_len, head_count, head_dim)

        def one_block(block_pair):
            block_query, block_index = block_pair
            scores = (
                jnp.einsum("qhe,khe->hqk", block_query, seq_key, preferred_element_type=jnp.float32)
                * score_scale
            )
            query_pos = block_index * block_len + jnp.arange(block_len, dtype=jnp.int32)
            allowed = (key_pos[None, :] <= query_pos[:, None]) & (key_pos[None, :] < length)
            scores = jnp.where(allowed[None], scores, -1e30)
            row_max = jnp.max(scores, axis=-1, keepdims=True)
            raised = jnp.exp(scores - row_max)
            weights = (raised / jnp.sum(raised, axis=-1, keepdims=True)).astype(jnp.bfloat16)
            return jnp.einsum(
                "hqk,khe->qhe", weights, seq_value, preferred_element_type=jnp.float32
            ).astype(jnp.bfloat16)

        results = lax.map(one_block, (blocks, jnp.arange(seq_len // block_len, dtype=jnp.int32)))
        return results.reshape(seq_len, head_count, head_dim)

    return lax.map(one_sequence, (queries, keys, values, lengths))


def write_cache(kv_cache, key_value, page_table, lengths):
    seq_count, page_count = page_table.shape
    page_len = kv_cache.shape[2]
    feat_here = kv_cache.shape[3]
    fresh_pages = jnp.moveaxis(key_value, 1, 0).reshape(
        2, seq_count * page_count, page_len, feat_here
    )
    slot_ids = page_table.reshape(-1)
    positions = (
        jnp.arange(page_count, dtype=jnp.int32)[:, None] * page_len
        + jnp.arange(page_len, dtype=jnp.int32)[None, :]
    )
    written = (positions[None] < lengths[:, None, None]).reshape(seq_count * page_count, page_len)
    current = kv_cache[:, slot_ids]
    new_pages = jnp.where(written[None, :, :, None], fresh_pages, current)
    return kv_cache.at[:, slot_ids].set(new_pages)


def body(tokens, ln_gain, ln_bias, w_qkv, b_qkv, w_out, b_out, kv_cache, page_table, lengths):
    model_width = tokens.shape[1]
    local_feat = w_qkv.shape[2]
    weights_flat = w_qkv.reshape(model_width, 3 * local_feat)
    bias_flat = b_qkv.reshape(-1)
    normed = layer_norm(tokens, ln_gain, ln_bias)
    block_rows = lax.all_gather(normed, "tp", axis=0, tiled=True)
    result = jnp.dot(block_rows, weights_flat, preferred_element_type=jnp.float32) + bias_flat
    projected = result.astype(jnp.bfloat16).reshape(block_rows.shape[0], 3, local_feat)
    all_rows = projected.shape[0]
    seq_len = all_rows // SEQS
    heads_here = local_feat // HD
    queries = projected[:, 0].reshape(SEQS, seq_len, heads_here, HD)
    keys = projected[:, 1].reshape(SEQS, seq_len, heads_here, HD)
    values = projected[:, 2].reshape(SEQS, seq_len, heads_here, HD)
    attended = attend(queries, keys, values, lengths).reshape(all_rows, local_feat)
    summed = lax.psum_scatter(
        jnp.dot(attended, w_out, preferred_element_type=jnp.float32).astype(jnp.bfloat16),
        "tp",
        scatter_dimension=0,
        tiled=True,
    ).astype(jnp.float32)
    attn_out = (summed + b_out).astype(jnp.bfloat16)
    kv_cache_out = write_cache(kv_cache, projected[:, 1:3], page_table, lengths)
    return (attn_out, kv_cache_out)


def solution(mesh):
    placed = (
        P(("dp", "tp"), None),
        P(),
        P(),
        P(None, None, "tp"),
        P(None, "tp"),
        P("tp", None),
        P(),
        P(None, "dp", None, "tp"),
        P("dp", None),
        P("dp"),
    )
    return jax.shard_map(
        body,
        mesh=mesh,
        in_specs=placed,
        out_specs=(P(("dp", "tp"), None), P(None, "dp", None, "tp")),
        check_vma=False,
    )
```

profile of v0, /device:TPU:0, one launch (start us, length us, event | category | flops | bytes accessed | tf_op | source)
XLA Modules:
  0.0 334.9 jit_solution(16525906927422556471)
XLA Ops:
  11.2 18.8 %copy.20 = bf16[6144,3,384]{0,2,1:T(8,128)(2,1)} copy(bf16[6144,3,384]{2,0,1:T(8,128)(2,1)} %param.15) | data formatting | bytes 28311552 | tf_op args[3]
  30.1 89.7 %all-gather.2.cloned.1.call-done = bf16[1280,6144]{1,0:T(8,128)(2,1)} async-done(((bf16[80,6144]{1,0:T(8,128)(2,1)}), bf16[1280,6144]{1,0:T(8,128)(2,1)}) %all-gather.2.cloned.1.call-update) | async-done | bytes 15728656 | tf_op jit(solution)/shard_map/all_gather | solution.py:77
  119.8 25.8 %fusion.37 = bf16[1280,1152]{0,1:T(8,128)(2,1)S(1)} fusion(bf16[1280,6144]{1,0:T(8,128)(2,1)} %all-gather.2.cloned.1.call-done, bf16[6144,1152]{0,1:T(8,128)(2,1)} %bitcast.67, f32[1152]{0:T(1024)S(1)} %add.87), kind=kOutput, calls=%fused_computation.32 | convolution fusion | flops 18122342400 | bytes 32838144 | tf_op jit(solution)/shard_map/dot_general | solution.py:78
  147.9 3.5 %reshape.187 = bf16[5,256,3,128]{1,0,3,2:T(8,128)(2,1)} reshape(bf16[1280,1,384]{0,2,1:T(8,128)(2,1)} %get-tuple-element.135) | data formatting | bytes 1966080 | tf_op jit(solution)/shard_map/while/body/eval_jaxpr/reshape | solution.py:29
  151.4 2.6 copy.22
  157.5 46.2 %while.19 = (s32[]{:T(128)}, bf16[5,256,3,128]{3,1,2,0:T(8,128)(2,1)}, s32[5]{0:T(128)S(1)}, s32[]{:T(128)}, bf16[5,256,3,128]{3,1,2,0:T(8,128)(2,1)}, /*index=5...) while((s32[]{:T(128)}, ...), condition=%wide.region_5.6_spmd.clone.clone, body=%wide.region_2.5_spmd.clone.clone.sunk | while | flops 764580608 | bytes 4534397 | solution.py:47
  159.5 2.9 fusion.72
  162.4 4.3 %fusion.73 = bf16[5,256,3,128]{3,1,2,0:T(8,128)(2,1)} fusion(bf16[5,256,3,128]{3,1,2,0:T(8,128)(2,1)} %get-tuple-element.189, s32[]{:T(128)} %get-tuple-element.188, bf16[1280,3,128]{2,0,1:T(8,128)(2,1)} %get-tuple-element.203, f32[3,256]{1,0:T(4,128)S(1)} %fusion.72, bf16[1280,3,128]{2,0,1:T(8,128)(2,1)} %get-tuple-element.202, ...), kind=kOutput, calls=%fused_computation.14.clone.1 | convolution fusion | flops 508332032 | bytes 2691072 | tf_op jit(solution)/shard_map/while/body/eval_jaxpr/while/body/eval_jaxpr/hqk,khe->qhe/dot_general | solution.py:43
  168.8 2.9 fusion.72
  171.6 4.3 %fusion.73 = bf16[5,256,3,128]{3,1,2,0:T(8,128)(2,1)} fusion(bf16[5,256,3,128]{3,1,2,0:T(8,128)(2,1)} %get-tuple-element.189, s32[]{:T(128)} %get-tuple-element.188, bf16[1280,3,128]{2,0,1:T(8,128)(2,1)} %get-tuple-element.203, f32[3,256]{1,0:T(4,128)S(1)} %fusion.72, bf16[1280,3,128]{2,0,1:T(8,128)(2,1)} %get-tuple-element.202, ...), kind=kOutput, calls=%fused_computation.14.clone.1 | convolution fusion | flops 508332032 | bytes 2691072 | tf_op jit(solution)/shard_map/while/body/eval_jaxpr/while/body/eval_jaxpr/hqk,khe->qhe/dot_general | solution.py:43
  178.0 2.9 fusion.72
  180.9 4.3 %fusion.73 = bf16[5,256,3,128]{3,1,2,0:T(8,128)(2,1)} fusion(bf16[5,256,3,128]{3,1,2,0:T(8,128)(2,1)} %get-tuple-element.189, s32[]{:T(128)} %get-tuple-element.188, bf16[1280,3,128]{2,0,1:T(8,128)(2,1)} %get-tuple-element.203, f32[3,256]{1,0:T(4,128)S(1)} %fusion.72, bf16[1280,3,128]{2,0,1:T(8,128)(2,1)} %get-tuple-element.202, ...), kind=kOutput, calls=%fused_computation.14.clone.1 | convolution fusion | flops 508332032 | bytes 2691072 | tf_op jit(solution)/shard_map/while/body/eval_jaxpr/while/body/eval_jaxpr/hqk,khe->qhe/dot_general | solution.py:43
  187.3 2.9 fusion.72
  190.1 4.3 %fusion.73 = bf16[5,256,3,128]{3,1,2,0:T(8,128)(2,1)} fusion(bf16[5,256,3,128]{3,1,2,0:T(8,128)(2,1)} %get-tuple-element.189, s32[]{:T(128)} %get-tuple-element.188, bf16[1280,3,128]{2,0,1:T(8,128)(2,1)} %get-tuple-element.203, f32[3,256]{1,0:T(4,128)S(1)} %fusion.72, bf16[1280,3,128]{2,0,1:T(8,128)(2,1)} %get-tuple-element.202, ...), kind=kOutput, calls=%fused_computation.14.clone.1 | convolution fusion | flops 508332032 | bytes 2691072 | tf_op jit(solution)/shard_map/while/body/eval_jaxpr/while/body/eval_jaxpr/hqk,khe->qhe/dot_general | solution.py:43
  196.5 2.9 fusion.72
  199.4 4.3 %fusion.73 = bf16[5,256,3,128]{3,1,2,0:T(8,128)(2,1)} fusion(bf16[5,256,3,128]{3,1,2,0:T(8,128)(2,1)} %get-tuple-element.189, s32[]{:T(128)} %get-tuple-element.188, bf16[1280,3,128]{2,0,1:T(8,128)(2,1)} %get-tuple-element.203, f32[3,256]{1,0:T(4,128)S(1)} %fusion.72, bf16[1280,3,128]{2,0,1:T(8,128)(2,1)} %get-tuple-element.202, ...), kind=kOutput, calls=%fused_computation.14.clone.1 | convolution fusion | flops 508332032 | bytes 2691072 | tf_op jit(solution)/shard_map/while/body/eval_jaxpr/while/body/eval_jaxpr/hqk,khe->qhe/dot_general | solution.py:43
  205.7 14.1 %convolution_convert_fusion = bf16[1280,6144]{1,0:T(8,128)(2,1)} fusion(bf16[384,6144]{1,0:T(8,128)(2,1)} %param.17, bf16[160,8,3,128]{3,2,1,0:T(4,128)(2,1)S(1)} %bitcast.73), kind=kOutput, calls=%fused_computation.30 | convolution fusion | flops 6047662080 | bytes 21430272 | tf_op jit(solution)/shard_map/dot_general | solution.py:88
  220.5 2.2 gather_fusion
  222.8 3.0 slice_bitcast_fusion
  225.8 4.0 %copy.26 = bf16[2,1280,384]{2,1,0:T(8,128)(2,1)} copy(bf16[2,1280,384]{1,2,0:T(8,128)(2,1)} %slice_bitcast_fusion) | data formatting | bytes 3932160 | tf_op jit(solution)/shard_map/transpose | solution.py:57
  229.8 3.7 %fusion.44 = bf16[10,2,128,384]{3,2,1,0:T(8,128)(2,1)} fusion(bf16[10,2,128,384]{3,2,1,0:T(8,128)(2,1)} %gather_fusion, bf16[2,10,128,384]{3,2,1,0:T(8,128)(2,1)} %bitcast.70, pred[10,128]{1,0:T(8,128)(4,1)S(1)} %add_compare_fusion), kind=kLoop, calls=%fused_computation.43 | loop fusion | flops 983040 | bytes 5899520 | tf_op jit(solution)/shard_map/jit(_where)/select_n | solution.py:67
  233.5 4.5 %scatter_fusion = bf16[2,12,128,384]{3,2,1,0:T(8,128)(2,1)S(1)} fusion(bf16[2,12,128,384]{3,2,1,0:T(8,128)(2,1)S(1)} %copy.47, s32[10]{0:T(128)S(1)} %fusion.47, bf16[10,2,128,384]{3,2,1,0:T(8,128)(2,1)} %fusion.44), kind=kCustom, calls=%fused_computation.1 | custom fusion | bytes 5898280 | tf_op jit(solution)/shard_map/scatter | solution.py:68
  238.0 87.7 %reduce-scatter.2.cloned.1.call-done = bf16[80,6144]{1,0:T(8,128)(2,1)} async-done(((bf16[1280,6144]{1,0:T(8,128)(2,1)}), bf16[80,6144]{1,0:T(8,128)(2,1)}) %reduce-scatter.2.cloned.1.call-update) | async-done | bytes 983056 | tf_op jit(solution)/shard_map/reduce_scatter | solution.py:87
  325.7 2.3 add_convert_fusion
  (57 shorter events, 19.5 us)
Async XLA Ops:
  7.2 1.9 copy-start.1
  7.2 2.6 copy-start.4
  7.2 2.6 copy-start.3
  7.2 112.6 %all-gather.2.cloned.1.call-start = ((), (), s32[]{:S(2)}) async-start(), calls=%async_computation.1 | async-start | bytes 16711680 | tf_op jit(solution)/shard_map/all_gather | solution.py:77
  11.2 314.5 %reduce-scatter.2.cloned.1.call-start = ((), (), s32[]{:S(2)}) async-start(), calls=%async_computation.2 | async-start | bytes 16711680 | tf_op jit(solution)/shard_map/reduce_scatter | solution.py:87
  11.2 18.8 %copy-start.6 = (f32[3,384]{1,0:T(4,128)S(1)}, f32[3,384]{1,0:T(4,128)}, u32[]{:S(2)}) copy-start(f32[3,384]{1,0:T(4,128)} %param.16) | copy-start | bytes 13828
  145.6 2.3 copy-start.2
  219.8 0.7 copy-start.7
  233.5 92.2 %copy-start.5 = (f32[6144]{0:T(1024)S(1)}, f32[6144]{0:T(1024)}, u32[]{:S(2)}) copy-start(f32[6144]{0:T(1024)} %param.18) | copy-start | bytes 73732
  238.0 90.0 %copy-start = (bf16[2,12,128,384]{3,2,1,0:T(8,128)(2,1)}, bf16[2,12,128,384]{3,2,1,0:T(8,128)(2,1)S(1)}, u32[]{:S(2)}) copy-start(bf16[2,12,128,384]{3,2,1,0:T(8,128)(2,1)S(1)} %scatter_fusion) | copy-start | bytes 7077892
Sparse Core Ops, SparseCore 0:
  11.3 108.4 all-gather.1
  219.9 105.7 reduce-scatter.1
where the time goes:
time: 336 us; the launch traced here: 335 us
  waiting for transfers between devices  177 us (53%)
  matrix products  75.7 us (23%)
  local copies, waits for them, and re-layouts  51 us (15%)
  between operations  14.8 us (4%)
  other arithmetic  12.9 us (4%)
    all_gather x1, waiting for transfers between devices, body(): block_rows = lax.all_gather(normed, 'tp', axis=0, tiled=True)  89.7 us
    reduce_scatter x1, waiting for transfers between devices, body(): lax.psum_scatter(jnp.dot(attended, w_out, preferred_element_type=jnp.floa...  87.7 us
    unnamed x21, local copies, waits for them, and re-layouts  27.4 us
    dot_general x1, matrix products, body(): jnp.dot(block_rows, weights_flat, preferred_element_type=jnp.float32)  25.8 us
    dot_general x5, matrix products, one_block(): jnp.einsum('hqk,khe->qhe', weights, seq_value, preferred_element_type=jnp...  21.6 us
    sub x5, matrix products, one_block(): raised = jnp.exp(scores - row_max)  14.3 us
    dot_general x1, matrix products, body(): jnp.dot(attended, w_out, preferred_element_type=jnp.float32)  14.1 us
    transpose x2, local copies, waits for them, and re-layouts, write_cache(): jnp.moveaxis(key_value, 1, 0)  6.97 us
  transfers between devices with their start and end apart: 2, of which 2 were waited for; matrix products, arithmetic and copies ran while one was open for 11% of the time, Pallas kernels for 0%

commit v1 on v0

--- a/solution.py
+++ b/solution.py
@@ -74,7 +74,14 @@
     weights_flat = w_qkv.reshape(model_width, 3 * local_feat)
     bias_flat = b_qkv.reshape(-1)
     normed = layer_norm(tokens, ln_gain, ln_bias)
-    block_rows = lax.all_gather(normed, "tp", axis=0, tiled=True)
+
+    def track_the_task(d_out, vals, bus_axis):
+        r_now = jnp.concatenate(
+            lax.all_to_all(jnp.stack(lax.axis_size(bus_axis) * [vals]), bus_axis, 0, 0), axis=d_out
+        )
+        return r_now
+
+    block_rows = track_the_task(0, vals=normed, bus_axis="tp")
     result = jnp.dot(block_rows, weights_flat, preferred_element_type=jnp.float32) + bias_flat
     projected = result.astype(jnp.bfloat16).reshape(block_rows.shape[0], 3, local_feat)
     all_rows = projected.shape[0]

time: 336 us -> 474 us (1.41)
  waiting for transfers between devices: 177 us -> 302 us
  starting transfers between devices: 0.08 us -> 8.07 us
  local copies, waits for them, and re-layouts: 51 us -> 56.9 us
    all_to_all x0 -> x1, waiting for transfers between devices: none -> 215 us  [track_the_task(): lax.all_to_all(jnp.stack(lax.axis_size(bus_axis) * [vals]), bus_axis, 0, 0)]
    all_gather x1 -> x0, waiting for transfers between devices: 89.7 us -> none  [body(): block_rows = lax.all_gather(normed, 'tp', axis=0, tiled=True)]
    all_to_all x0 -> x1, starting transfers between devices: none -> 8.03 us  [track_the_task(): lax.all_to_all(jnp.stack(lax.axis_size(bus_axis) * [vals]), bus_axis, 0, 0)]
    another operation x0 -> x1, local copies, waits for them, and re-layouts: none -> 5.66 us  [track_the_task(): jnp.stack(lax.axis_size(bus_axis) * [vals])]
  transfers between devices with their start and end apart: 2 -> 2, of which waited for: 2 -> 2; matrix products, arithmetic and copies ran while one was open for 11% -> 8% of each run, Pallas kernels for 0% -> 0%
where the time goes in v1:
time: 474 us; the launch traced here: 472 us
  waiting for transfers between devices  302 us (64%)
  matrix products  75.7 us (16%)
  local copies, waits for them, and re-layouts  56.9 us (12%)
  between operations  14.8 us (3%)
  other arithmetic  11.9 us (3%)
  starting transfers between devices  8.07 us (2%)
    all_to_all x1, waiting for transfers between devices, track_the_task(): lax.all_to_all(jnp.stack(lax.axis_size(bus_axis) * [vals]), bus_axis, 0, 0)  215 us
    reduce_scatter x1, waiting for transfers between devices, body(): lax.psum_scatter(jnp.dot(attended, w_out, preferred_element_type=jnp.floa...  86.1 us
    unnamed x21, local copies, waits for them, and re-layouts  27.3 us
    dot_general x1, matrix products, body(): jnp.dot(block_rows, weights_flat, preferred_element_type=jnp.float32)  25.8 us
    dot_general x5, matrix products, one_block(): jnp.einsum('hqk,khe->qhe', weights, seq_value, preferred_element_type=jnp...  21.6 us
    sub x5, matrix products, one_block(): raised = jnp.exp(scores - row_max)  14.3 us
    dot_general x1, matrix products, body(): jnp.dot(attended, w_out, preferred_element_type=jnp.float32)  14.1 us
  transfers between devices with their start and end apart: 2, of which 2 were waited for; matrix products, arithmetic and copies ran while one was open for 8% of the time, Pallas kernels for 0%

profile of v1, /device:TPU:0, one launch (start us, length us, event | category | flops | bytes accessed | tf_op | source)
XLA Modules:
  0.0 472.4 jit_solution(556247978357589500)
XLA Ops:
  10.2 5.7 %stack.2 = bf16[16,80,6144]{2,1,0:T(8,128)(2,1)} broadcast(bf16[80,6144]{1,0:T(8,128)(2,1)S(1)} %fusion.43), dimensions={1,2} | broadcast | bytes 16711680 | tf_op jit(solution)/shard_map/stack | solution.py:80
  15.9 8.0 %all-to-all-start = ((bf16[16,80,6144]{2,1,0:T(8,128)(2,1)}), bf16[16,80,6144]{2,1,0:T(8,128)(2,1)}, u32[]{:S(2)}, u32[]{:S(2)}) async-start(bf16[16,80,6144]{2,1,0:T(8,128)(2,1)} %stack.2), calls=%async_computation | async-start | bytes 31457280 | tf_op jit(solution)/shard_map/all_to_all | solution.py:80
  24.0 18.7 %copy.20 = bf16[6144,3,384]{0,2,1:T(8,128)(2,1)} copy(bf16[6144,3,384]{2,0,1:T(8,128)(2,1)} %param.15) | data formatting | bytes 28311552 | tf_op args[3]
  42.7 215.5 %all-to-all-done = bf16[16,80,6144]{2,1,0:T(8,128)(2,1)} async-done(((bf16[16,80,6144]{2,1,0:T(8,128)(2,1)}), bf16[16,80,6144]{2,1,0:T(8,128)(2,1)}, u32[]{:S(2)}, u32[]{:S(2)}) %all-to-all-start) | async-done | bytes 15728672 | tf_op jit(solution)/shard_map/all_to_all | solution.py:80
  258.1 25.8 %fusion.37 = bf16[1280,1152]{0,1:T(8,128)(2,1)S(1)} fusion(bf16[1280,6144]{1,0:T(8,128)(2,1)} %bitcast.1, bf16[6144,1152]{0,1:T(8,128)(2,1)} %bitcast.68, f32[1152]{0:T(1024)S(1)} %add.87), kind=kOutput, calls=%fused_computation.32 | convolution fusion | flops 18122342400 | bytes 32838144 | tf_op jit(solution)/shard_map/dot_general | solution.py:85
  286.3 3.5 reshape.193
  289.7 2.6 copy.22
  295.8 46.9 %while.19 = (s32[]{:T(128)}, bf16[5,256,3,128]{3,1,2,0:T(8,128)(2,1)}, s32[5]{0:T(128)S(1)}, s32[]{:T(128)}, bf16[5,256,3,128]{3,1,2,0:T(8,128)(2,1)}, /*index=5...) while((s32[]{:T(128)}, ...), condition=%wide.region_5.6_spmd.clone.clone, body=%wide.region_2.5_spmd.clone.clone.sunk | while | flops 764580608 | bytes 4534397 | solution.py:47
  298.0 2.9 fusion.72
  300.9 4.3 fusion.73
  307.4 2.9 fusion.72
  310.2 4.3 fusion.73
  316.8 2.9 fusion.72
  319.6 4.3 fusion.73
  326.2 2.9 fusion.72
  329.0 4.3 fusion.73
  335.5 2.9 fusion.72
  338.4 4.3 fusion.73
  344.8 14.1 %convolution_convert_fusion = bf16[1280,6144]{1,0:T(8,128)(2,1)} fusion(bf16[384,6144]{1,0:T(8,128)(2,1)} %param.17, bf16[160,8,3,128]{3,2,1,0:T(4,128)(2,1)S(1)} %bitcast.74), kind=kOutput, calls=%fused_computation.30 | convolution fusion | flops 6047662080 | bytes 21430272 | tf_op jit(solution)/shard_map/dot_general | solution.py:95
  361.8 3.0 slice_bitcast_fusion
  364.8 4.0 copy.26
  368.9 3.7 fusion.44
  372.6 4.5 scatter_fusion
  377.1 86.1 %reduce-scatter.2.cloned.1.call-done = bf16[80,6144]{1,0:T(8,128)(2,1)} async-done(((bf16[1280,6144]{1,0:T(8,128)(2,1)}), bf16[80,6144]{1,0:T(8,128)(2,1)}) %reduce-scatter.2.cloned.1.call-update) | async-done | bytes 983056 | tf_op jit(solution)/shard_map/reduce_scatter | solution.py:94
  (57 shorter events, 23.3 us)
Async XLA Ops:
  7.2 1.9 copy-start.1
  7.2 2.6 copy-start.4
  7.2 2.6 copy-start.3
  15.9 242.3 %all-to-all-start = ((bf16[16,80,6144]{2,1,0:T(8,128)(2,1)}), bf16[16,80,6144]{2,1,0:T(8,128)(2,1)}, u32[]{:S(2)}, u32[]{:S(2)}) async-start(bf16[16,80,6144]{2,1,0:T(8,128)(2,1)} %stack.2), calls=%async_computation | async-start | bytes 31457280 | tf_op jit(solution)/shard_map/all_to_all | solution.py:80
  23.9 439.3 %reduce-scatter.2.cloned.1.call-start = ((), (), s32[]{:S(2)}) async-start(), calls=%async_computation.2 | async-start | bytes 16711680 | tf_op jit(solution)/shard_map/reduce_scatter | solution.py:94
  24.0 18.7 %copy-start.6 = (f32[3,384]{1,0:T(4,128)S(1)}, f32[3,384]{1,0:T(4,128)}, u32[]{:S(2)}) copy-start(f32[3,384]{1,0:T(4,128)} %param.16) | copy-start | bytes 13828
  283.9 2.3 copy-start.2
  358.8 0.7 copy-start.7
  372.6 90.6 %copy-start.5 = (f32[6144]{0:T(1024)S(1)}, f32[6144]{0:T(1024)}, u32[]{:S(2)}) copy-start(f32[6144]{0:T(1024)} %param.18) | copy-start | bytes 73732
  377.1 88.4 %copy-start = (bf16[2,12,128,384]{3,2,1,0:T(8,128)(2,1)}, bf16[2,12,128,384]{3,2,1,0:T(8,128)(2,1)S(1)}, u32[]{:S(2)}) copy-start(bf16[2,12,128,384]{3,2,1,0:T(8,128)(2,1)S(1)} %scatter_fusion) | copy-start | bytes 7077892
Sparse Core Ops, SparseCore 0:
  359.0 104.2 reduce-scatter.1
